TPU v7x, 1024 devices: a whole 4x4x32 slice. The times are simulated.
1024 devices in a mesh: sp: 32 (over y, x, core), dp: 32 (over z).
Axes of the slice: x: 4, y: 4, z: 32, core: 2. Of those that a mesh axis runs over, the one named last changes fastest.
Arguments:
- hidden: bfloat16 [32, 8192, 4096], P('dp', 'sp'), may hold values from -24 to 24
- pad_counts: int32 [32, 32], P('dp', 'sp'), may hold values from 64 to 128
- doc_lengths: int32 [32, 128], P('dp'), may hold values from 1 to 128, 8192 in all within a row
- range_shift: int32 [32, 32], P('dp'), may hold values from -32 to 32
- qkv_weight: bfloat16 [4096, 384], P('dp'), may hold values from -0.09375 to 0.09375
Outputs:
- attended: bfloat16 [32, 8192, 128], P('dp', 'sp')
Inputs may be any that keep to these rules, and one draw needn't show every extreme that they name: `doc_lengths`: each row sums to 8192.
All inputs are finite; a program needn't handle non-finite values.
Results may differ from a plain program's by a relative error of at most 0.0095.
Values may be sent and summed in bfloat16 or wider, within the bound.
No kernel may reach another device: no remote copies, remote signals or barrier semaphores. Data moves between devices by JAX's collectives and lax.ppermute only.
A program may use at most 32 MiB of HBM per device.

v0:
```python
import math

import jax
import jax.numpy as jnp
from jax import lax
from jax.experimental import pallas as pl
from jax.experimental.pallas import tpu as pltpu
from jax.sharding import Mesh
from jax.sharding import PartitionSpec as P

PLANE = ("y", "x", "core")
EDGE = 32
SIDE = 4
NEAR = [d for k in range(8) for _ in range(2) for d in ((k, -k) if k else (0, 8))]
FAR = [d for k in range(8) for _ in range(2) for d in ((16 - k, k - 16) if k else (16, -8))]
SHIFTS = (NEAR, FAR)
SMALL = pltpu.CompilerParams(vmem_limit_bytes=16 * 1024 * 1024)


def project_half(side, plane, sources, block):
    lanes = block.shape[2]
    planes = sources[0].shape[1] // lanes
    deep = (block.shape[1] - 8) // 6
    total = None
    for pair in range(block.shape[0] // 2):
        inputs, weights = [], []
        for kind in range(2):
            north, south = (SHIFTS[kind][4 * pair + c] for c in range(2))
            shard = lax.rem(plane + planes - jnp.where(side == 0, north, south), planes)
            columns = pl.ds(pl.multiple_of(shard * lanes, lanes), lanes)
            inputs.append(jnp.concatenate([rows[:, columns] for rows in sources], axis=0))
            at = kind * 3 * deep
            for chip in (2 * pair, 2 * pair + 1):
                weights.append(
                    jnp.concatenate(
                        [block[chip, at + i * deep : at + (i + 1) * deep] for i in range(3)],
                        axis=1,
                    )
                )
        part = jnp.dot(
            jnp.concatenate(inputs, axis=1),
            jnp.concatenate(weights, axis=0),
            preferred_element_type=jnp.float32,
        )
        total = part if total is None else total + part
    return total


def tokens_before(side, index, block):
    last = block.shape[1] - 8
    total = jnp.zeros((8, block.shape[2]), jnp.float32)
    for chip in range(block.shape[0]):
        owner = jnp.where(side == 0, device(chip, 0), device(chip, 1))
        total += jnp.where(owner < index, block[chip, last:].astype(jnp.float32), 0.0)
    return total


def project_kernel(scalars, slots, left, right, half, projected, before):
    side, plane, index = (scalars[i] for i in range(4, 7))
    projected[...] = project_half(side, plane, (slots, left, right), half)
    before[...] = tokens_before(side, index, half)


def project(scalars, slots, left, right, half):
    rows = slots.shape[0] + left.shape[0] + right.shape[0]
    chips, deep, lanes = half.shape[0], (half.shape[1] - 8) // 6, half.shape[2]
    return pl.pallas_call(
        project_kernel,
        out_shape=(
            jax.ShapeDtypeStruct((rows, 3 * lanes), jnp.float32),
            jax.ShapeDtypeStruct((8, lanes), jnp.float32),
        ),
        in_specs=[pl.BlockSpec(memory_space=pltpu.SMEM)]
        + [pl.BlockSpec(memory_space=pltpu.VMEM)] * 4,
        out_specs=(pl.BlockSpec(memory_space=pltpu.VMEM),) * 2,
        compiler_params=SMALL,
        cost_estimate=pl.CostEstimate(
            flops=12 * rows * chips * deep * lanes, bytes_accessed=0, transcendentals=0
        ),
        name="project",
    )(scalars, slots, left, right, half)


def attend_kernel(
    scalars, slots, left, right, projected, before, other, ends, attended
):
    rows, head_dim = attended.shape
    padding, held, shift, count, side, plane, index = (scalars[i] for i in range(7))
    before = before[...] + tokens_before(1 - side, index, other)
    start = before[:1, :1].astype(jnp.int32) + shift
    sources = (slots, left, right)
    projected = (projected[...] + project_half(1 - side, plane, sources, other)).astype(
        jnp.bfloat16
    )
    row = lax.broadcasted_iota(jnp.int32, (rows, 1), 0)
    live = row < count
    offset = row + shift
    source = jnp.where(
        offset < 0,
        rows + EDGE + offset,
        jnp.where(offset < held, padding + offset, rows + EDGE + offset - held),
    )
    source = jnp.where(live, source, -1)
    columns = lax.broadcasted_iota(jnp.int32, (rows, projected.shape[0]), 1)
    picked = jnp.where(columns == source, 1.0, 0.0).astype(jnp.bfloat16)
    projected = jnp.dot(picked, projected, preferred_element_type=jnp.float32).astype(
        jnp.bfloat16
    )
    query, keys, values = (projected[:, i * head_dim : (i + 1) * head_dim] for i in range(3))
    scores = lax.dot_general(
        query, keys, (((1,), (1,)), ((), ())), preferred_element_type=jnp.float32
    ) / math.sqrt(head_dim)
    key = lax.broadcasted_iota(jnp.int32, (rows, rows), 1)
    passed = jnp.where(ends[...] <= row + start, ends[...], 0)
    opened = jnp.max(passed, axis=1, keepdims=True) - start
    allowed = (key <= row) & (key >= opened) & live
    masked = jnp.where(allowed, scores, -1e30)
    peak = jnp.max(masked, axis=1, keepdims=True)
    exponent = jnp.where(allowed, jnp.exp(masked - peak), 0.0)
    denominator = jnp.sum(exponent, axis=1, keepdims=True)
    probs = (exponent / jnp.where(live, denominator, 1.0)).astype(jnp.bfloat16)
    result = jnp.dot(probs, values, preferred_element_type=jnp.float32)
    attended[...] = jnp.where(live, result, 0.0).astype(jnp.bfloat16)


def attend(scalars, slots, left, right, projected, before, other, ends):
    return pl.pallas_call(
        attend_kernel,
        out_shape=jax.ShapeDtypeStruct((slots.shape[0], other.shape[2]), jnp.bfloat16),
        in_specs=[pl.BlockSpec(memory_space=pltpu.SMEM)]
        + [pl.BlockSpec(memory_space=pltpu.VMEM)] * 7,
        out_specs=pl.BlockSpec(memory_space=pltpu.VMEM),
        compiler_params=SMALL,
        name="attend",
    )(scalars, slots, left, right, projected, before, other, ends)


def for_each(value, count):
    return jnp.broadcast_to(value[None], (count, *value.shape))


def device(place, side):
    chip = place if side == 0 else place % SIDE * SIDE + place // SIDE
    return 2 * chip + (side + chip % SIDE + chip // SIDE) % 2


def moved(value, kind):
    planes = lax.axis_size("z")
    pairs = [
        (device(place, side) * planes + z, device(place, side) * planes + (z + shift) % planes)
        for place in range(SIDE * SIDE)
        for side, shift in enumerate(SHIFTS[kind][2 * place : 2 * place + 2])
        for z in range(planes)
    ]
    return lax.ppermute(value, (*PLANE, "z"), pairs)


def spread(value, step):
    lines = [[SIDE * i + at for at in range(SIDE)] for i in range(SIDE)]
    if step:
        lines = [list(line) for line in zip(*lines)]
    groups = [[device(place, side) for place in line] for line in lines for side in range(2)]
    return lax.all_to_all(
        for_each(value, SIDE), PLANE, 0, 0, axis_index_groups=groups, tiled=True
    )


def shards(hidden, pad_counts, doc_lengths, range_shift, qkv_weight):
    slots = hidden[0]
    rows = slots.shape[0]
    size, index = lax.axis_size(PLANE), lax.axis_index(PLANE)
    padding = pad_counts[0, 0]
    live = rows - padding

    deep = qkv_weight.shape[0] // 2
    x, y = lax.axis_index("x"), lax.axis_index("y")
    side = (lax.axis_index("core") + x + y) % 2
    upper = jnp.where(side == 0, x, y) % 2
    own = lax.dynamic_slice_in_dim(qkv_weight, upper * deep, deep, 0)
    own = jnp.concatenate(jnp.split(own, 3, axis=1), axis=0)
    far = moved(own, 1)
    head = lax.dynamic_slice_in_dim(slots, padding, EDGE, 0)
    tail = slots[rows - EDGE :]
    left = lax.ppermute(tail, PLANE, [(i, i + 1) for i in range(size - 1)])
    right = lax.ppermute(head, PLANE, [(i + 1, i) for i in range(size - 1)])
    near = moved(own, 0)

    shifts = range_shift[0]
    shift = jnp.where(index == 0, 0, shifts[index])
    following = jnp.where(index == size - 1, 0, shifts[jnp.minimum(index + 1, size - 1)])
    count = live + following - shift
    ends = jnp.cumsum(doc_lengths[0])[None]
    scalars = jnp.stack(
        [padding, live, shift, count, side, lax.axis_index("z"), index]
    ).astype(jnp.int32)
    near, far, ends, scalars = lax.optimization_barrier((near, far, ends, scalars))
    tally = jnp.full((8, own.shape[1]), live).astype(jnp.bfloat16)
    line = spread(jnp.concatenate([near, far, tally]), 0)
    half = spread(line, 1).reshape(-1, *line.shape[1:])
    other = lax.ppermute(half, "core", [(0, 1), (1, 0)])
    projected, before = project(scalars, slots, left, right, half)
    return attend(scalars, slots, left, right, projected, before, other, ends)[None]


def solution(mesh):
    fine = Mesh(mesh.devices.reshape(4, 4, 2, -1), ("y", "x", "core", "z"))
    in_specs = (P("z", PLANE, None), P("z", PLANE), P("z", None), P("z", None), P("z", None))
    return jax.shard_map(
        shards, mesh=fine, in_specs=in_specs, out_specs=P("z", PLANE, None), check_vma=False
    )
```

profile of v0, /device:TPU:7, one launch (start us, length us, event | category | flops | bytes accessed | tf_op | source)
XLA Modules:
  0.0 91.4 jit_solution(12918439139930573406)
XLA Ops:
  0.0 0.8 constant_dynamic-slice_fusion
  0.8 3.5 %collective-permute-start = (bf16[192,128]{1,0:T(8,128)(2,1)S(1)}, bf16[192,128]{1,0:T(8,128)(2,1)S(1)}, u32[]{:S(2)}, u32[]{:S(2)}) collective-permute-start(bf16[192,128]{1,0:T(8,128)(2,1)S(1)} %pad_maximum_fusion), channel_id=1, source_target_pairs={{0,0},{1,1},{2,2},{3,3},{4,4},{5,5},{6,6},{7,7},{8,8},{9,9},{10,10... | collective-permute-start | bytes 147464 | tf_op jit(solution)/shard_map/ppermute | solution.py:155
  4.3 27.3 %collective-permute-start.1 = (bf16[192,128]{1,0:T(8,128)(2,1)S(1)}, bf16[192,128]{1,0:T(8,128)(2,1)S(1)}, u32[]{:S(2)}, u32[]{:S(2)}) collective-permute-start(bf16[192,128]{1,0:T(8,128)(2,1)S(1)} %pad_maximum_fusion), channel_id=1, source_target_pairs={{0,16},{1,17},{2,18},{3,19},{4,20},{5,21},{6,22},{7,23},{8,24},{9,... | collective-permute-start | bytes 147464 | tf_op jit(solution)/shard_map/ppermute | solution.py:155
  32.3 1.3 %constant_dynamic-slice_fusion.1 = (s32[1,1]{1,0:T(1,128)}, s32[1,1]{1,0:T(1,128)}) fusion(s32[1,32]{1,0:T(1,128)} %param.8, s32[]{:T(128)S(6)} %select_n.39, s32[]{:T(128)S(6)} %select_n.37), kind=kLoop, calls=%fused_computation.5 | loop fusion | bytes 24 | tf_op jit(solution)/shard_map/dynamic_slice | solution.py:190
  34.3 1.0 %reduce-window_clone.1.ends = s32[1,128]{1,0:T(1,128)S(1)} reduce-window(s32[1,128]{1,0:T(1,128)} %param.7, s32[]{:T(128)} %constant.46.clone.1), window={size=1x128 pad=0_0x127_0}, to_apply=%region_0.1 | reduce-window | flops 16256 | bytes 1028 | tf_op jit(solution)/shard_map/reduce-window.clone
  36.0 0.1 stack.27.scalars
  36.0 0.0 collective-permute-done
  36.0 0.0 collective-permute-done.1
  36.0 0.1 maximum_maximum_fusion
  36.2 0.1 broadcast_in_dim.9
  36.2 10.2 %all_to_all.10 = bf16[4,392,128]{2,1,0:T(8,128)(2,1)S(1)} all-to-all(bf16[4,392,128]{2,1,0:T(8,128)(2,1)S(1)} %broadcast_in_dim.9), channel_id=1, replica_groups={{0,96,128,224},{32,256,544,768},{288,320,416,448},{64,352,576,864},{512..., dimensions={0} | all-to-all | bytes 802816 | tf_op jit(solution)/shard_map/all_to_all | solution.py:163
  46.4 0.2 broadcast_in_dim.10
  46.6 0.0 copy-start
  46.7 17.6 %all_to_all.11 = bf16[4,4,392,128]{3,2,1,0:T(8,128)(2,1)} all-to-all(bf16[4,4,392,128]{3,2,1,0:T(8,128)(2,1)S(1)} %broadcast_in_dim.10), channel_id=1, replica_groups={{0,288,512,800},{32,64,160,192},{96,320,608,832},{256,352,384,480},{128..., dimensions={0} | all-to-all | bytes 3211264 | tf_op jit(solution)/shard_map/all_to_all | solution.py:163
  64.3 7.1 %collective-permute-start.4 = (bf16[16,392,128]{2,1,0:T(8,128)(2,1)}, bf16[16,392,128]{2,1,0:T(8,128)(2,1)}, u32[]{:S(2)}, u32[]{:S(2)}) collective-permute-start(bf16[16,392,128]{2,1,0:T(8,128)(2,1)} %bitcast.13.half), channel_id=1, source_target_pairs={{0,32},{32,0},{1,33},{33,1},{2,34},{34,2},{3,35},{35,3},{4,36},{36... | collective-permute-start | bytes 4816904 | tf_op jit(solution)/shard_map/ppermute | solution.py:200
  71.4 0.0 copy-done
  71.4 0.1 dynamic-slice_bitcast_fusion
  71.5 4.1 %collective-permute-start.2 = (bf16[32,4096]{1,0:T(8,128)(2,1)S(1)}, bf16[32,4096]{1,0:T(8,128)(2,1)S(1)}, u32[]{:S(2)}, u32[]{:S(2)}) collective-permute-start(bf16[32,4096]{1,0:T(8,128)(2,1)S(1)} %get-tuple-element.18), channel_id=1, source_target_pairs={{0,32},{32,64},{64,96},{96,128},{128,160},{160,192},{192,224},{224... | collective-permute-start | bytes 786440 | tf_op jit(solution)/shard_map/ppermute | solution.py:184
  75.6 1.9 %collective-permute-start.3 = (bf16[32,4096]{1,0:T(8,128)(2,1)S(1)}, bf16[32,4096]{1,0:T(8,128)(2,1)S(1)}, u32[]{:S(2)}, u32[]{:S(2)}) collective-permute-start(bf16[32,4096]{1,0:T(8,128)(2,1)S(1)} %get-tuple-element.17), channel_id=1, source_target_pairs={{32,0},{64,32},{96,64},{128,96},{160,128},{192,160},{224,192},{256... | collective-permute-start | bytes 786440 | tf_op jit(solution)/shard_map/ppermute | solution.py:185
  77.5 1.4 %collective-permute-done.2.left = bf16[32,4096]{1,0:T(8,128)(2,1)S(1)} collective-permute-done((bf16[32,4096]{1,0:T(8,128)(2,1)S(1)}, bf16[32,4096]{1,0:T(8,128)(2,1)S(1)}, u32[]{:S(2)}, u32[]{:S(2)}) %collective-permute-start.2) | collective-permute-done | bytes 262176 | tf_op jit(solution)/shard_map/ppermute | solution.py:184
  78.9 6.5 %collective-permute-done.3.right = bf16[32,4096]{1,0:T(8,128)(2,1)S(1)} collective-permute-done((bf16[32,4096]{1,0:T(8,128)(2,1)S(1)}, bf16[32,4096]{1,0:T(8,128)(2,1)S(1)}, u32[]{:S(2)}, u32[]{:S(2)}) %collective-permute-start.3) | collective-permute-done | bytes 262176 | tf_op jit(solution)/shard_map/ppermute | solution.py:185
  85.4 2.3 %project.1 = (f32[320,384]{1,0:T(8,128)S(1)}, f32[8,128]{1,0:T(8,128)S(1)}) custom-call(s32[7]{0:T(128)S(1)} %stack.27.scalars, bf16[256,4096]{1,0:T(8,128)(2,1)S(1)} %bitcast.22, bf16[32,4096]{1,0:T(8,128)(2,1)S(1)} %collective-permute-done.2.left, bf16[32,4096]{1,0:T(8,128)(2,1)S(1)} %collective-permute-done.3.right, bf16[16,392,128]{2,1,0:T(8,128)(2,1)} %bitcast.13.half), custom_call_target="tpu_custom_call" | custom-call | flops 503316480 | tf_op jit(solution)/shard_map/project/pallas_call | solution.py:67
  87.7 0.0 collective-permute-done.4.other
  87.7 3.7 %attend.1 = bf16[256,128]{1,0:T(8,128)(2,1)} custom-call(s32[7]{0:T(128)S(1)} %stack.27.scalars, bf16[256,4096]{1,0:T(8,128)(2,1)S(1)} %bitcast.23, bf16[32,4096]{1,0:T(8,128)(2,1)S(1)} %collective-permute-done.2.left, bf16[32,4096]{1,0:T(8,128)(2,1)S(1)} %collective-permute-done.3.right, f32[320,384]{1,0:T(8,128)S(1)} %get-tuple-element.14.projected, ...), custom_call_target="tpu_custom_call" | custom-call | tf_op jit(solution)/shard_map/attend/pallas_call | solution.py:127
  (3 shorter events, 0.0 us)
Async XLA Ops:
  0.8 35.3 %collective-permute-start = (bf16[192,128]{1,0:T(8,128)(2,1)S(1)}, bf16[192,128]{1,0:T(8,128)(2,1)S(1)}, u32[]{:S(2)}, u32[]{:S(2)}) collective-permute-start(bf16[192,128]{1,0:T(8,128)(2,1)S(1)} %pad_maximum_fusion), channel_id=1, source_target_pairs={{0,0},{1,1},{2,2},{3,3},{4,4},{5,5},{6,6},{7,7},{8,8},{9,9},{10,10... | collective-permute-start | bytes 147464 | tf_op jit(solution)/shard_map/ppermute | solution.py:155
  4.3 31.7 %collective-permute-start.1 = (bf16[192,128]{1,0:T(8,128)(2,1)S(1)}, bf16[192,128]{1,0:T(8,128)(2,1)S(1)}, u32[]{:S(2)}, u32[]{:S(2)}) collective-permute-start(bf16[192,128]{1,0:T(8,128)(2,1)S(1)} %pad_maximum_fusion), channel_id=1, source_target_pairs={{0,16},{1,17},{2,18},{3,19},{4,20},{5,21},{6,22},{7,23},{8,24},{9,... | collective-permute-start | bytes 147464 | tf_op jit(solution)/shard_map/ppermute | solution.py:155
  46.6 24.8 %copy-start = (bf16[1,256,4096]{2,1,0:T(8,128)(2,1)S(1)}, bf16[1,256,4096]{2,1,0:T(8,128)(2,1)}, u32[]{:S(2)}) copy-start(bf16[1,256,4096]{2,1,0:T(8,128)(2,1)} %param.5) | copy-start | bytes 6291460
  64.3 23.4 %collective-permute-start.4 = (bf16[16,392,128]{2,1,0:T(8,128)(2,1)}, bf16[16,392,128]{2,1,0:T(8,128)(2,1)}, u32[]{:S(2)}, u32[]{:S(2)}) collective-permute-start(bf16[16,392,128]{2,1,0:T(8,128)(2,1)} %bitcast.13.half), channel_id=1, source_target_pairs={{0,32},{32,0},{1,33},{33,1},{2,34},{34,2},{3,35},{35,3},{4,36},{36... | collective-permute-start | bytes 4816904 | tf_op jit(solution)/shard_map/ppermute | solution.py:200
  71.5 7.4 %collective-permute-start.2 = (bf16[32,4096]{1,0:T(8,128)(2,1)S(1)}, bf16[32,4096]{1,0:T(8,128)(2,1)S(1)}, u32[]{:S(2)}, u32[]{:S(2)}) collective-permute-start(bf16[32,4096]{1,0:T(8,128)(2,1)S(1)} %get-tuple-element.18), channel_id=1, source_target_pairs={{0,32},{32,64},{64,96},{96,128},{128,160},{160,192},{192,224},{224... | collective-permute-start | bytes 786440 | tf_op jit(solution)/shard_map/ppermute | solution.py:184
  75.6 9.8 %collective-permute-start.3 = (bf16[32,4096]{1,0:T(8,128)(2,1)S(1)}, bf16[32,4096]{1,0:T(8,128)(2,1)S(1)}, u32[]{:S(2)}, u32[]{:S(2)}) collective-permute-start(bf16[32,4096]{1,0:T(8,128)(2,1)S(1)} %get-tuple-element.17), channel_id=1, source_target_pairs={{32,0},{64,32},{96,64},{128,96},{160,128},{192,160},{224,192},{256... | collective-permute-start | bytes 786440 | tf_op jit(solution)/shard_map/ppermute | solution.py:185
where the time goes:
time: 91.8 us; the launch traced here: 91.4 us
  starting transfers between devices  44 us (48%)
  blocking collectives  27.8 us (30%)
  waiting for transfers between devices  7.88 us (9%)
  Pallas kernels  5.98 us (7%)
  local copies, waits for them, and re-layouts  2.54 us (3%)
  between operations  2.08 us (2%)
  other arithmetic  1.08 us (1%)
    ppermute x2, starting transfers between devices, moved(): return lax.ppermute(value, (*PLANE, 'z'), pairs)  30.9 us
    all_to_all x2, blocking collectives, spread(): lax.all_to_all(for_each(value, SIDE), PLANE, 0, 0, axis_index_groups=grou...  27.8 us
    ppermute x1, starting transfers between devices, shards(): other = lax.ppermute(half, 'core', [(0, 1), (1, 0)])  7.08 us
    ppermute x1, waiting for transfers between devices, shards(): right = lax.ppermute(head, PLANE, [(i + 1, i) for i in range(size - 1)])  6.51 us
    ppermute x1, starting transfers between devices, shards(): left = lax.ppermute(tail, PLANE, [(i, i + 1) for i in range(size - 1)])  4.07 us
    pallas_call x1, Pallas kernels, attend(): pl.pallas_call(attend_kernel, out_shape=jax.ShapeDtypeStruct((slots.shape...  3.7 us
    pallas_call x1, Pallas kernels, project(): pl.pallas_call(project_kernel, out_shape=(jax.ShapeDtypeStruct((rows, 3 *...  2.28 us
    ppermute x1, starting transfers between devices, shards(): right = lax.ppermute(head, PLANE, [(i + 1, i) for i in range(size - 1)])  1.92 us
  transfers between devices with their start and end apart: 5, of which 2 were waited for; matrix products, arithmetic and copies ran while one was open for 3% of the time, Pallas kernels for 2%

commit v1 on v0

v1 whole, which is shorter than its diff:
```python
import math

import jax
import jax.numpy as jnp
from jax import lax
from jax.experimental import pallas as pl
from jax.experimental.pallas import tpu as pltpu
from jax.sharding import Mesh
from jax.sharding import PartitionSpec as P

PLANE = ("y", "x", "core")
EDGE = 32
SIDE = 4
STEPS = (0, 1, 3, 2)
NEAR = [d for k in range(8) for _ in range(2) for d in ((k, -k) if k else (0, 8))]
FAR = [d for k in range(8) for _ in range(2) for d in ((16 - k, k - 16) if k else (16, -8))]
SHIFTS = (NEAR, FAR)
SMALL = pltpu.CompilerParams(vmem_limit_bytes=16 * 1024 * 1024)


def distance(k, side, kind):
    if kind == 0:
        return jnp.where(side == 0, k, jnp.where(k == 0, 8, -k))
    return jnp.where(side == 0, 16 - k, jnp.where(k == 0, -8, k - 16))


def project_half(side, at, plane, sources, blocks):
    lanes = blocks[0].shape[2]
    planes = sources[0].shape[1] // lanes
    deep = (blocks[0].shape[1] - 8) // 6
    total = None
    for step, block in zip(STEPS, blocks):
        line = lax.rem(at + SIDE - step, SIDE)
        for pair in range(SIDE // 2):
            inputs, weights = [], []
            for kind in range(2):
                shift = distance(SIDE // 2 * line + pair, side, kind)
                shard = lax.rem(plane + planes - shift, planes)
                columns = pl.ds(pl.multiple_of(shard * lanes, lanes), lanes)
                inputs.append(jnp.concatenate([rows[:, columns] for rows in sources], axis=0))
                first = kind * 3 * deep
                for place in (2 * pair, 2 * pair + 1):
                    weights.append(
                        jnp.concatenate(
                            [
                                block[place, first + i * deep : first + (i + 1) * deep]
                                for i in range(3)
                            ],
                            axis=1,
                        )
                    )
            part = jnp.dot(
                jnp.concatenate(inputs, axis=1),
                jnp.concatenate(weights, axis=0),
                preferred_element_type=jnp.float32,
            )
            total = part if total is None else total + part
    return total


def tokens_before(side, at, index, blocks):
    last = blocks[0].shape[1] - 8
    total = jnp.zeros((8, blocks[0].shape[2]), jnp.float32)
    for step, block in zip(STEPS, blocks):
        line = lax.rem(at + SIDE - step, SIDE)
        for place in range(SIDE):
            chip = jnp.where(side == 0, SIDE * line + place, SIDE * place + line)
            owner = 2 * chip + lax.rem(side + line + place, 2)
            total += jnp.where(owner < index, block[place, last:].astype(jnp.float32), 0.0)
    return total


def project_kernel(scalars, slots, left, right, *rest):
    blocks, (projected, before) = rest[:SIDE], rest[SIDE:]
    side, at, plane, index = (scalars[i] for i in (4, 5, 7, 8))
    projected[...] = project_half(side, at, plane, (slots, left, right), blocks)
    before[...] = tokens_before(side, at, index, blocks)


def project(scalars, slots, left, right, blocks):
    rows = slots.shape[0] + left.shape[0] + right.shape[0]
    lanes = blocks[0].shape[2]
    return pl.pallas_call(
        project_kernel,
        out_shape=(
            jax.ShapeDtypeStruct((rows, 3 * lanes), jnp.float32),
            jax.ShapeDtypeStruct((8, lanes), jnp.float32),
        ),
        in_specs=[pl.BlockSpec(memory_space=pltpu.SMEM)]
        + [pl.BlockSpec(memory_space=pltpu.VMEM)] * (3 + SIDE),
        out_specs=(pl.BlockSpec(memory_space=pltpu.VMEM),) * 2,
        compiler_params=SMALL,
        cost_estimate=pl.CostEstimate(
            flops=3 * rows * slots.shape[1] * lanes, bytes_accessed=0, transcendentals=0
        ),
        name="project",
    )(scalars, slots, left, right, *blocks)


def attend_kernel(scalars, slots, left, right, projected, before, ends, *rest):
    blocks, attended = rest[:SIDE], rest[SIDE]
    rows, head_dim = attended.shape
    padding, held, shift, count, side, _, at, plane, index = (scalars[i] for i in range(9))
    before = before[...] + tokens_before(1 - side, at, index, blocks)
    start = before[:1, :1].astype(jnp.int32) + shift
    sources = (slots, left, right)
    projected = (projected[...] + project_half(1 - side, at, plane, sources, blocks)).astype(
        jnp.bfloat16
    )
    row = lax.broadcasted_iota(jnp.int32, (rows, 1), 0)
    live = row < count
    offset = row + shift
    source = jnp.where(
        offset < 0,
        rows + EDGE + offset,
        jnp.where(offset < held, padding + offset, rows + EDGE + offset - held),
    )
    source = jnp.where(live, source, -1)
    columns = lax.broadcasted_iota(jnp.int32, (rows, projected.shape[0]), 1)
    picked = jnp.where(columns == source, 1.0, 0.0).astype(jnp.bfloat16)
    projected = jnp.dot(picked, projected, preferred_element_type=jnp.float32).astype(
        jnp.bfloat16
    )
    query, keys, values = (projected[:, i * head_dim : (i + 1) * head_dim] for i in range(3))
    scores = lax.dot_general(
        query, keys, (((1,), (1,)), ((), ())), preferred_element_type=jnp.float32
    ) / math.sqrt(head_dim)
    key = lax.broadcasted_iota(jnp.int32, (rows, rows), 1)
    passed = jnp.where(ends[...] <= row + start, ends[...], 0)
    opened = jnp.max(passed, axis=1, keepdims=True) - start
    allowed = (key <= row) & (key >= opened) & live
    masked = jnp.where(allowed, scores, -1e30)
    peak = jnp.max(masked, axis=1, keepdims=True)
    exponent = jnp.where(allowed, jnp.exp(masked - peak), 0.0)
    denominator = jnp.sum(exponent, axis=1, keepdims=True)
    probs = (exponent / jnp.where(live, denominator, 1.0)).astype(jnp.bfloat16)
    result = jnp.dot(probs, values, preferred_element_type=jnp.float32)
    attended[...] = jnp.where(live, result, 0.0).astype(jnp.bfloat16)


def attend(scalars, slots, left, right, projected, before, ends, blocks):
    return pl.pallas_call(
        attend_kernel,
        out_shape=jax.ShapeDtypeStruct((slots.shape[0], ends.shape[1]), jnp.bfloat16),
        in_specs=[pl.BlockSpec(memory_space=pltpu.SMEM)]
        + [pl.BlockSpec(memory_space=pltpu.VMEM)] * (6 + SIDE),
        out_specs=pl.BlockSpec(memory_space=pltpu.VMEM),
        compiler_params=SMALL,
        name="attend",
    )(scalars, slots, left, right, projected, before, ends, *blocks)


def for_each(value, count):
    return jnp.broadcast_to(value[None], (count, *value.shape))


def device(place, side):
    chip = place if side == 0 else place % SIDE * SIDE + place // SIDE
    return 2 * chip + (side + chip % SIDE + chip // SIDE) % 2


def moved(value, kind):
    planes = lax.axis_size("z")
    pairs = [
        (device(place, side) * planes + z, device(place, side) * planes + (z + shift) % planes)
        for place in range(SIDE * SIDE)
        for side, shift in enumerate(SHIFTS[kind][2 * place : 2 * place + 2])
        for z in range(planes)
    ]
    return lax.ppermute(value, (*PLANE, "z"), pairs)


def line_of(value):
    groups = [
        [device(SIDE * at + place, side) for place in range(SIDE)]
        for at in range(SIDE)
        for side in range(2)
    ]
    return lax.all_to_all(
        for_each(value, SIDE), PLANE, 0, 0, axis_index_groups=groups, tiled=True
    )


def passed_on(value, step):
    pairs = [
        (device(place, side), device((place + SIDE * step) % SIDE**2, side))
        for place in range(SIDE**2)
        for side in range(2)
    ]
    return lax.ppermute(value, PLANE, pairs)


def shards(hidden, pad_counts, doc_lengths, range_shift, qkv_weight):
    slots = hidden[0]
    rows = slots.shape[0]
    size, index = lax.axis_size(PLANE), lax.axis_index(PLANE)
    padding = pad_counts[0, 0]
    live = rows - padding

    deep = qkv_weight.shape[0] // 2
    x, y = lax.axis_index("x"), lax.axis_index("y")
    side = (lax.axis_index("core") + x + y) % 2
    upper = jnp.where(side == 0, x, y) % 2
    own = lax.dynamic_slice_in_dim(qkv_weight, upper * deep, deep, 0)
    own = jnp.concatenate(jnp.split(own, 3, axis=1), axis=0)
    far = moved(own, 1)
    head = lax.dynamic_slice_in_dim(slots, padding, EDGE, 0)
    tail = slots[rows - EDGE :]
    left = lax.ppermute(tail, PLANE, [(i, i + 1) for i in range(size - 1)])
    right = lax.ppermute(head, PLANE, [(i + 1, i) for i in range(size - 1)])
    near = moved(own, 0)

    shifts = range_shift[0]
    shift = jnp.where(index == 0, 0, shifts[index])
    following = jnp.where(index == size - 1, 0, shifts[jnp.minimum(index + 1, size - 1)])
    count = live + following - shift
    ends = jnp.cumsum(doc_lengths[0])[None]
    scalars = jnp.stack(
        [
            padding,
            live,
            shift,
            count,
            side,
            jnp.where(side == 0, y, x),
            jnp.where(side == 0, x, y),
            lax.axis_index("z"),
            index,
        ]
    ).astype(jnp.int32)
    tally = jnp.full((8, own.shape[1]), live).astype(jnp.bfloat16)
    blocks = [line_of(jnp.concatenate([near, far, tally]))]
    for step in STEPS[1:]:
        blocks.append(passed_on(blocks[0], step))
    blocks[-1], ends, scalars = lax.optimization_barrier((blocks[-1], ends, scalars))
    others = []
    for step, block in zip(STEPS, blocks):
        others.append(lax.ppermute(block, "core", [(0, 1), (1, 0)]))
    projected, before = project(scalars, slots, left, right, blocks)
    return attend(scalars, slots, left, right, projected, before, ends, others)[None]


def solution(mesh):
    fine = Mesh(mesh.devices.reshape(4, 4, 2, -1), ("y", "x", "core", "z"))
    in_specs = (P("z", PLANE, None), P("z", PLANE), P("z", None), P("z", None), P("z", None))
    return jax.shard_map(
        shards, mesh=fine, in_specs=in_specs, out_specs=P("z", PLANE, None), check_vma=False
    )
```

time: 91.8 us -> 93.6 us (1.020)
  blocking collectives: 27.8 us -> 0 us
  starting transfers between devices: 44 us -> 67.9 us
  waiting for transfers between devices: 7.88 us -> 13.5 us
  local copies, waits for them, and re-layouts: 2.54 us -> 4.27 us
  Pallas kernels: 5.98 us -> 4.8 us
    all_to_all x2 -> x0, blocking collectives: 27.8 us -> none  [spread(): lax.all_to_all(for_each(value, SIDE), PLANE, 0, 0, axis_index_groups=grou...]
    ppermute x1 -> x7, starting transfers between devices: 7.08 us -> 18.3 us  [the longest x3 9.61 us: passed_on(): return lax.ppermute(value, PLANE, pairs)]
    all_to_all x0 -> x1, starting transfers between devices: none -> 8.04 us  [line_of(): lax.all_to_all(for_each(value, SIDE), PLANE, 0, 0, axis_index_groups=grou...]
    all_to_all x0 -> x1, waiting for transfers between devices: none -> 4.48 us  [line_of(): lax.all_to_all(for_each(value, SIDE), PLANE, 0, 0, axis_index_groups=grou...]
    ppermute x1, starting transfers between devices: 4.07 us -> 8.23 us  [shards(): left = lax.ppermute(tail, PLANE, [(i, i + 1) for i in range(size - 1)])]
    dynamic_slice x1, local copies, waits for them, and re-layouts: 0.07 us -> 1.8 us  [shards(): head = lax.dynamic_slice_in_dim(slots, padding, EDGE, 0)]
    ppermute x2, waiting for transfers between devices: 0.01 us -> 1.63 us  [moved(): return lax.ppermute(value, (*PLANE, 'z'), pairs)]
    ppermute x1, waiting for transfers between devices: 1.37 us -> 0.01 us  [shards(): left = lax.ppermute(tail, PLANE, [(i, i + 1) for i in range(size - 1)])]
  transfers between devices with their start and end apart: 5 -> 12, of which waited for: 2 -> 3; matrix products, arithmetic and copies ran while one was open for 3% -> 3% of each run, Pallas kernels for 2% -> 2%
where the time goes in v1:
time: 93.6 us; the launch traced here: 93.1 us
  starting transfers between devices  67.9 us (73%)
  waiting for transfers between devices  13.5 us (14%)
  Pallas kernels  4.8 us (5%)
  local copies, waits for them, and re-layouts  4.27 us (5%)
  between operations  2.19 us (2%)
    ppermute x2, starting transfers between devices, moved(): return lax.ppermute(value, (*PLANE, 'z'), pairs)  30.9 us
    ppermute x3, starting transfers between devices, passed_on(): return lax.ppermute(value, PLANE, pairs)  9.61 us
    ppermute x4, starting transfers between devices, shards(): others.append(lax.ppermute(block, 'core', [(0, 1), (1, 0)]))  8.71 us
    ppermute x1, starting transfers between devices, shards(): left = lax.ppermute(tail, PLANE, [(i, i + 1) for i in range(size - 1)])  8.23 us
    all_to_all x1, starting transfers between devices, line_of(): lax.all_to_all(for_each(value, SIDE), PLANE, 0, 0, axis_index_groups=grou...  8.04 us
    ppermute x1, waiting for transfers between devices, shards(): right = lax.ppermute(head, PLANE, [(i + 1, i) for i in range(size - 1)])  7.39 us
    all_to_all x1, waiting for transfers between devices, line_of(): lax.all_to_all(for_each(value, SIDE), PLANE, 0, 0, axis_index_groups=grou...  4.48 us
    pallas_call x1, Pallas kernels, attend(): pl.pallas_call(attend_kernel, out_shape=jax.ShapeDtypeStruct((slots.shape...  2.82 us
  transfers between devices with their start and end apart: 12, of which 3 were waited for; matrix products, arithmetic and copies ran while one was open for 3% of the time, Pallas kernels for 2%

profile of v1, /device:TPU:7, one launch (start us, length us, event | category | flops | bytes accessed | tf_op | source)
XLA Modules:
  0.0 93.1 jit_solution(15894950165248626211)
XLA Ops:
  0.0 0.9 constant_dynamic-slice_fusion
  1.0 26.1 %collective-permute-start.1 = (bf16[192,128]{1,0:T(8,128)(2,1)S(1)}, bf16[192,128]{1,0:T(8,128)(2,1)S(1)}, u32[]{:S(2)}, u32[]{:S(2)}) collective-permute-start(bf16[192,128]{1,0:T(8,128)(2,1)S(1)} %pad_maximum_fusion), channel_id=1, source_target_pairs={{0,16},{1,17},{2,18},{3,19},{4,20},{5,21},{6,22},{7,23},{8,24},{9,... | collective-permute-start | bytes 147464 | tf_op jit(solution)/shard_map/ppermute | solution.py:170
  27.1 4.8 %collective-permute-start = (bf16[192,128]{1,0:T(8,128)(2,1)S(1)}, bf16[192,128]{1,0:T(8,128)(2,1)S(1)}, u32[]{:S(2)}, u32[]{:S(2)}) collective-permute-start(bf16[192,128]{1,0:T(8,128)(2,1)S(1)} %pad_maximum_fusion), channel_id=1, source_target_pairs={{0,0},{1,1},{2,2},{3,3},{4,4},{5,5},{6,6},{7,7},{8,8},{9,9},{10,10... | collective-permute-start | bytes 147464 | tf_op jit(solution)/shard_map/ppermute | solution.py:170
  32.5 0.0 collective-permute-done.1
  32.5 1.6 %collective-permute-done = bf16[192,128]{1,0:T(8,128)(2,1)S(1)} collective-permute-done((bf16[192,128]{1,0:T(8,128)(2,1)S(1)}, bf16[192,128]{1,0:T(8,128)(2,1)S(1)}, u32[]{:S(2)}, u32[]{:S(2)}) %collective-permute-start) | collective-permute-done | bytes 49184 | tf_op jit(solution)/shard_map/ppermute | solution.py:170
  34.2 0.1 maximum_maximum_fusion
  34.3 0.8 broadcast_in_dim.14
  35.1 8.0 %all-to-all-start = ((bf16[4,392,128]{2,1,0:T(8,128)(2,1)}), bf16[4,392,128]{2,1,0:T(8,128)(2,1)S(1)}, u32[]{:S(2)}, u32[]{:S(2)}) async-start(bf16[4,392,128]{2,1,0:T(8,128)(2,1)} %broadcast_in_dim.14), calls=%async_computation | async-start | bytes 802816 | tf_op jit(solution)/shard_map/all_to_all | solution.py:179
  43.1 4.5 %all-to-all-done.rest_0_ = bf16[4,392,128]{2,1,0:T(8,128)(2,1)S(1)} async-done(((bf16[4,392,128]{2,1,0:T(8,128)(2,1)}), bf16[4,392,128]{2,1,0:T(8,128)(2,1)S(1)}, u32[]{:S(2)}, u32[]{:S(2)}) %all-to-all-start) | async-done | bytes 401440 | tf_op jit(solution)/shard_map/all_to_all | solution.py:179
  47.6 2.8 %collective-permute-start.2 = (bf16[4,392,128]{2,1,0:T(8,128)(2,1)S(1)}, bf16[4,392,128]{2,1,0:T(8,128)(2,1)S(1)}, u32[]{:S(2)}, u32[]{:S(2)}) collective-permute-start(bf16[4,392,128]{2,1,0:T(8,128)(2,1)S(1)} %all-to-all-done.rest_0_), channel_id=1, source_target_pairs={{0,512},{32,160},{96,608},{256,384},{128,640},{544,672},{224,736},... | collective-permute-start | bytes 1204232 | tf_op jit(solution)/shard_map/ppermute | solution.py:190
  50.5 4.0 %collective-permute-start.5 = (bf16[4,392,128]{2,1,0:T(8,128)(2,1)S(1)}, bf16[4,392,128]{2,1,0:T(8,128)(2,1)}, u32[]{:S(2)}, u32[]{:S(2)}) collective-permute-start(bf16[4,392,128]{2,1,0:T(8,128)(2,1)S(1)} %all-to-all-done.rest_0_), channel_id=1, source_target_pairs={{0,288},{32,64},{96,320},{256,352},{128,416},{544,576},{224,448},{... | collective-permute-start | bytes 1204232 | tf_op jit(solution)/shard_map/ppermute | solution.py:190
  54.5 2.7 %collective-permute-start.6 = (bf16[4,392,128]{2,1,0:T(8,128)(2,1)S(1)}, bf16[4,392,128]{2,1,0:T(8,128)(2,1)}, u32[]{:S(2)}, u32[]{:S(2)}) collective-permute-start(bf16[4,392,128]{2,1,0:T(8,128)(2,1)S(1)} %all-to-all-done.rest_0_), channel_id=1, source_target_pairs={{0,800},{32,192},{96,832},{256,480},{128,928},{544,704},{224,960},... | collective-permute-start | bytes 1204232 | tf_op jit(solution)/shard_map/ppermute | solution.py:190
  57.3 1.8 %dynamic-slice_bitcast_fusion = (bf16[32,4096]{1,0:T(8,128)(2,1)S(1)}, bf16[32,4096]{1,0:T(8,128)(2,1)}) fusion(bf16[1,256,4096]{2,1,0:T(8,128)(2,1)} %param.5, s32[]{:T(128)S(6)} %select_n.46), kind=kLoop, calls=%fused_computation | loop fusion | bytes 1048580 | tf_op jit(solution)/shard_map/dynamic_slice | solution.py:207
  59.1 8.2 %collective-permute-start.3 = (bf16[32,4096]{1,0:T(8,128)(2,1)}, bf16[32,4096]{1,0:T(8,128)(2,1)S(1)}, u32[]{:S(2)}, u32[]{:S(2)}) collective-permute-start(bf16[32,4096]{1,0:T(8,128)(2,1)} %get-tuple-element.16), channel_id=1, source_target_pairs={{0,32},{32,64},{64,96},{96,128},{128,160},{160,192},{192,224},{224... | collective-permute-start | bytes 786440 | tf_op jit(solution)/shard_map/ppermute | solution.py:209
  67.3 0.3 reduce-window_clone.1.ends
  67.7 0.6 constant_dynamic-slice_fusion.1
  69.6 0.1 stack.35.scalars
  69.7 2.5 %collective-permute-start.7 = (bf16[4,392,128]{2,1,0:T(8,128)(2,1)S(1)}, bf16[4,392,128]{2,1,0:T(8,128)(2,1)S(1)}, u32[]{:S(2)}, u32[]{:S(2)}) collective-permute-start(bf16[4,392,128]{2,1,0:T(8,128)(2,1)S(1)} %all-to-all-done.rest_0_), channel_id=1, source_target_pairs={{0,32},{32,0},{1,33},{33,1},{2,34},{34,2},{3,35},{35,3},{4,36},{36... | collective-permute-start | bytes 1204232 | tf_op jit(solution)/shard_map/ppermute | solution.py:238
  72.1 0.0 collective-permute-done.2.rest_3_
  72.1 0.0 collective-permute-done.5.rest_1_
  72.2 1.9 %collective-permute-start.8 = (bf16[4,392,128]{2,1,0:T(8,128)(2,1)}, bf16[4,392,128]{2,1,0:T(8,128)(2,1)S(1)}, u32[]{:S(2)}, u32[]{:S(2)}) collective-permute-start(bf16[4,392,128]{2,1,0:T(8,128)(2,1)} %collective-permute-done.5.rest_1_), channel_id=1, source_target_pairs={{0,32},{32,0},{1,33},{33,1},{2,34},{34,2},{3,35},{35,3},{4,36},{36... | collective-permute-start | bytes 1204232 | tf_op jit(solution)/shard_map/ppermute | solution.py:238
  74.1 0.0 collective-permute-done.6.rest_2_
  74.1 2.4 %collective-permute-start.9 = (bf16[4,392,128]{2,1,0:T(8,128)(2,1)}, bf16[4,392,128]{2,1,0:T(8,128)(2,1)S(1)}, u32[]{:S(2)}, u32[]{:S(2)}) collective-permute-start(bf16[4,392,128]{2,1,0:T(8,128)(2,1)} %collective-permute-done.6.rest_2_), channel_id=1, source_target_pairs={{0,32},{32,0},{1,33},{33,1},{2,34},{34,2},{3,35},{35,3},{4,36},{36... | collective-permute-start | bytes 1204232 | tf_op jit(solution)/shard_map/ppermute | solution.py:238
  76.5 1.9 %collective-permute-start.10 = (bf16[4,392,128]{2,1,0:T(8,128)(2,1)S(1)}, bf16[4,392,128]{2,1,0:T(8,128)(2,1)S(1)}, u32[]{:S(2)}, u32[]{:S(2)}) collective-permute-start(bf16[4,392,128]{2,1,0:T(8,128)(2,1)S(1)} %collective-permute-done.2.rest_3_), channel_id=1, source_target_pairs={{0,32},{32,0},{1,33},{33,1},{2,34},{34,2},{3,35},{35,3},{4,36},{36... | collective-permute-start | bytes 1204232 | tf_op jit(solution)/shard_map/ppermute | solution.py:238
  78.4 0.0 collective-permute-done.3.left
  78.4 2.4 %collective-permute-start.4 = (bf16[32,4096]{1,0:T(8,128)(2,1)S(1)}, bf16[32,4096]{1,0:T(8,128)(2,1)S(1)}, u32[]{:S(2)}, u32[]{:S(2)}) collective-permute-start(bf16[32,4096]{1,0:T(8,128)(2,1)S(1)} %get-tuple-element.15), channel_id=1, source_target_pairs={{32,0},{64,32},{96,64},{128,96},{160,128},{192,160},{224,192},{256... | collective-permute-start | bytes 786440 | tf_op jit(solution)/shard_map/ppermute | solution.py:210
  80.9 7.4 %collective-permute-done.4.right = bf16[32,4096]{1,0:T(8,128)(2,1)S(1)} collective-permute-done((bf16[32,4096]{1,0:T(8,128)(2,1)S(1)}, bf16[32,4096]{1,0:T(8,128)(2,1)S(1)}, u32[]{:S(2)}, u32[]{:S(2)}) %collective-permute-start.4) | collective-permute-done | bytes 262176 | tf_op jit(solution)/shard_map/ppermute | solution.py:210
  88.2 2.0 %project.1 = (f32[320,384]{1,0:T(8,128)S(1)}, f32[8,128]{1,0:T(8,128)S(1)}) custom-call(s32[9]{0:T(128)S(1)} %stack.35.scalars, bf16[256,4096]{1,0:T(8,128)(2,1)S(1)} %bitcast.23, bf16[32,4096]{1,0:T(8,128)(2,1)S(1)} %collective-permute-done.3.left, bf16[32,4096]{1,0:T(8,128)(2,1)S(1)} %collective-permute-done.4.right, ...), custom_call_target="tpu_custom_call" | custom-call | flops 503316480 | tf_op jit(solution)/shard_map/project/pallas_call | solution.py:83
  90.2 0.0 collective-permute-done.7.rest_0_
  90.2 0.0 collective-permute-done.8.rest_1_
  90.3 0.0 collective-permute-done.9.rest_2_
  90.3 2.8 %attend.1 = bf16[256,128]{1,0:T(8,128)(2,1)} custom-call(s32[9]{0:T(128)S(1)} %stack.35.scalars, bf16[256,4096]{1,0:T(8,128)(2,1)S(1)} %bitcast.24, bf16[32,4096]{1,0:T(8,128)(2,1)S(1)} %collective-permute-done.3.left, bf16[32,4096]{1,0:T(8,128)(2,1)S(1)} %collective-permute-done.4.right, f32[320,384]{1,0:T(8,128)S(1)} %get-tuple-element.12.projected, ...), custom_call_target="tpu_custom_call" | custom-call | tf_op jit(solution)/shard_map/attend/pallas_call | solution.py:142
  (10 shorter events, 0.0 us)
Async XLA Ops:
  0.0 88.2 %copy-start = (bf16[1,256,4096]{2,1,0:T(8,128)(2,1)S(1)}, bf16[1,256,4096]{2,1,0:T(8,128)(2,1)}, u32[]{:S(2)}) copy-start(bf16[1,256,4096]{2,1,0:T(8,128)(2,1)} %param.5) | copy-start | bytes 6291460
  0.0 67.3 %copy-start.2 = (s32[1,128]{1,0:T(1,128)S(1)}, s32[1,128]{1,0:T(1,128)}, u32[]{:S(2)}) copy-start(s32[1,128]{1,0:T(1,128)} %param.7) | copy-start | bytes 1540
  0.0 67.6 %copy-start.1 = (s32[1,32]{1,0:T(1,128)S(1)}, s32[1,32]{1,0:T(1,128)}, u32[]{:S(2)}) copy-start(s32[1,32]{1,0:T(1,128)} %param.8) | copy-start | bytes 388
  1.0 31.6 %collective-permute-start.1 = (bf16[192,128]{1,0:T(8,128)(2,1)S(1)}, bf16[192,128]{1,0:T(8,128)(2,1)S(1)}, u32[]{:S(2)}, u32[]{:S(2)}) collective-permute-start(bf16[192,128]{1,0:T(8,128)(2,1)S(1)} %pad_maximum_fusion), channel_id=1, source_target_pairs={{0,16},{1,17},{2,18},{3,19},{4,20},{5,21},{6,22},{7,23},{8,24},{9,... | collective-permute-start | bytes 147464 | tf_op jit(solution)/shard_map/ppermute | solution.py:170
  27.1 7.1 %collective-permute-start = (bf16[192,128]{1,0:T(8,128)(2,1)S(1)}, bf16[192,128]{1,0:T(8,128)(2,1)S(1)}, u32[]{:S(2)}, u32[]{:S(2)}) collective-permute-start(bf16[192,128]{1,0:T(8,128)(2,1)S(1)} %pad_maximum_fusion), channel_id=1, source_target_pairs={{0,0},{1,1},{2,2},{3,3},{4,4},{5,5},{6,6},{7,7},{8,8},{9,9},{10,10... | collective-permute-start | bytes 147464 | tf_op jit(solution)/shard_map/ppermute | solution.py:170
  35.1 12.5 %all-to-all-start = ((bf16[4,392,128]{2,1,0:T(8,128)(2,1)}), bf16[4,392,128]{2,1,0:T(8,128)(2,1)S(1)}, u32[]{:S(2)}, u32[]{:S(2)}) async-start(bf16[4,392,128]{2,1,0:T(8,128)(2,1)} %broadcast_in_dim.14), calls=%async_computation | async-start | bytes 802816 | tf_op jit(solution)/shard_map/all_to_all | solution.py:179
  47.6 24.5 %collective-permute-start.2 = (bf16[4,392,128]{2,1,0:T(8,128)(2,1)S(1)}, bf16[4,392,128]{2,1,0:T(8,128)(2,1)S(1)}, u32[]{:S(2)}, u32[]{:S(2)}) collective-permute-start(bf16[4,392,128]{2,1,0:T(8,128)(2,1)S(1)} %all-to-all-done.rest_0_), channel_id=1, source_target_pairs={{0,512},{32,160},{96,608},{256,384},{128,640},{544,672},{224,736},... | collective-permute-start | bytes 1204232 | tf_op jit(solution)/shard_map/ppermute | solution.py:190
  50.5 21.7 %collective-permute-start.5 = (bf16[4,392,128]{2,1,0:T(8,128)(2,1)S(1)}, bf16[4,392,128]{2,1,0:T(8,128)(2,1)}, u32[]{:S(2)}, u32[]{:S(2)}) collective-permute-start(bf16[4,392,128]{2,1,0:T(8,128)(2,1)S(1)} %all-to-all-done.rest_0_), channel_id=1, source_target_pairs={{0,288},{32,64},{96,320},{256,352},{128,416},{544,576},{224,448},{... | collective-permute-start | bytes 1204232 | tf_op jit(solution)/shard_map/ppermute | solution.py:190
  54.5 19.6 %collective-permute-start.6 = (bf16[4,392,128]{2,1,0:T(8,128)(2,1)S(1)}, bf16[4,392,128]{2,1,0:T(8,128)(2,1)}, u32[]{:S(2)}, u32[]{:S(2)}) collective-permute-start(bf16[4,392,128]{2,1,0:T(8,128)(2,1)S(1)} %all-to-all-done.rest_0_), channel_id=1, source_target_pairs={{0,800},{32,192},{96,832},{256,480},{128,928},{544,704},{224,960},... | collective-permute-start | bytes 1204232 | tf_op jit(solution)/shard_map/ppermute | solution.py:190
  59.1 19.4 %collective-permute-start.3 = (bf16[32,4096]{1,0:T(8,128)(2,1)}, bf16[32,4096]{1,0:T(8,128)(2,1)S(1)}, u32[]{:S(2)}, u32[]{:S(2)}) collective-permute-start(bf16[32,4096]{1,0:T(8,128)(2,1)} %get-tuple-element.16), channel_id=1, source_target_pairs={{0,32},{32,64},{64,96},{96,128},{128,160},{160,192},{192,224},{224... | collective-permute-start | bytes 786440 | tf_op jit(solution)/shard_map/ppermute | solution.py:209
  69.7 20.6 %collective-permute-start.7 = (bf16[4,392,128]{2,1,0:T(8,128)(2,1)S(1)}, bf16[4,392,128]{2,1,0:T(8,128)(2,1)S(1)}, u32[]{:S(2)}, u32[]{:S(2)}) collective-permute-start(bf16[4,392,128]{2,1,0:T(8,128)(2,1)S(1)} %all-to-all-done.rest_0_), channel_id=1, source_target_pairs={{0,32},{32,0},{1,33},{33,1},{2,34},{34,2},{3,35},{35,3},{4,36},{36... | collective-permute-start | bytes 1204232 | tf_op jit(solution)/shard_map/ppermute | solution.py:238
  72.2 18.1 %collective-permute-start.8 = (bf16[4,392,128]{2,1,0:T(8,128)(2,1)}, bf16[4,392,128]{2,1,0:T(8,128)(2,1)S(1)}, u32[]{:S(2)}, u32[]{:S(2)}) collective-permute-start(bf16[4,392,128]{2,1,0:T(8,128)(2,1)} %collective-permute-done.5.rest_1_), channel_id=1, source_target_pairs={{0,32},{32,0},{1,33},{33,1},{2,34},{34,2},{3,35},{35,3},{4,36},{36... | collective-permute-start | bytes 1204232 | tf_op jit(solution)/shard_map/ppermute | solution.py:238
  74.1 16.2 %collective-permute-start.9 = (bf16[4,392,128]{2,1,0:T(8,128)(2,1)}, bf16[4,392,128]{2,1,0:T(8,128)(2,1)S(1)}, u32[]{:S(2)}, u32[]{:S(2)}) collective-permute-start(bf16[4,392,128]{2,1,0:T(8,128)(2,1)} %collective-permute-done.6.rest_2_), channel_id=1, source_target_pairs={{0,32},{32,0},{1,33},{33,1},{2,34},{34,2},{3,35},{35,3},{4,36},{36... | collective-permute-start | bytes 1204232 | tf_op jit(solution)/shard_map/ppermute | solution.py:238
  76.5 13.8 %collective-permute-start.10 = (bf16[4,392,128]{2,1,0:T(8,128)(2,1)S(1)}, bf16[4,392,128]{2,1,0:T(8,128)(2,1)S(1)}, u32[]{:S(2)}, u32[]{:S(2)}) collective-permute-start(bf16[4,392,128]{2,1,0:T(8,128)(2,1)S(1)} %collective-permute-done.2.rest_3_), channel_id=1, source_target_pairs={{0,32},{32,0},{1,33},{33,1},{2,34},{34,2},{3,35},{35,3},{4,36},{36... | collective-permute-start | bytes 1204232 | tf_op jit(solution)/shard_map/ppermute | solution.py:238
  78.4 9.8 %collective-permute-start.4 = (bf16[32,4096]{1,0:T(8,128)(2,1)S(1)}, bf16[32,4096]{1,0:T(8,128)(2,1)S(1)}, u32[]{:S(2)}, u32[]{:S(2)}) collective-permute-start(bf16[32,4096]{1,0:T(8,128)(2,1)S(1)} %get-tuple-element.15), channel_id=1, source_target_pairs={{32,0},{64,32},{96,64},{128,96},{160,128},{192,160},{224,192},{256... | collective-permute-start | bytes 786440 | tf_op jit(solution)/shard_map/ppermute | solution.py:210
